TPU v7x, 32 devices: a whole 2x2x4 slice. The times are simulated.
32 devices in a mesh: grp: 8 (over z, x), row: 4 (over y, core).
Axes of the slice: x: 2, y: 2, z: 4, core: 2. Of those that a mesh axis runs over, the one named last changes fastest.
Arguments:
- gll_state: float32 [8, 32, 16, 4096], P(None, None, None, ('grp', 'row')), may hold values from -6 to 6
- metric: float32 [16, 4096], P(None, ('grp', 'row')), may hold values from 0.7 to 1.4
- phys_owner: int32 [4096, 4, 1], P(('grp', 'row')), may hold values from 0 to 7; in each aligned block of 512 rows (0 to 511, 512 to 1023, ..., all dimensions but the last counted through in order) at most 128 rows name the same one
- neighbours: int32 [4, 4096], P(None, ('grp', 'row')), may hold values from 0 to 4095, as said below
- phys_rate: float32 [32, 32768], P(None, ('grp', 'row')), may hold values from 0.2 to 2
- phys_forcing: float32 [32, 32768], P(None, ('grp', 'row')), may hold values from -6 to 6
- field_mix: float32 [8, 8], replicated, may hold values from -2 to 2
Outputs:
- gll_tend: float32 [8, 32, 16, 4096], P(None, None, None, ('grp', 'row'))
Inputs may be any that keep to these rules, and one draw needn't show every extreme that they name: `phys_owner`: in the 512 rows of one device, no owner is named more than 128 times, and some owner reaches 128. `neighbours`: rows 0 and 1 of element e are e - 1 and e + 1, cyclically over 4096 elements; rows 2 and 3 lie 2 to 32 positions before and after e, cyclically, and some element has a neighbour exactly 32 positions away.
All inputs are finite; a program needn't handle non-finite values.
Results may differ from a plain program's by a relative error of at most 0.000094.
Values sent between devices are 32-bit elements; how exact they have to be, the bound alone decides.
No kernel may reach another device: no remote copies, remote signals or barrier semaphores. Data moves between devices by JAX's collectives and lax.ppermute only.
A program may use at most 64 MiB of HBM per device.

v0:
```python
import jax
import jax.numpy as jnp
import numpy as np
from jax import lax
from jax.sharding import PartitionSpec as P

HALO = 32


def padded_2(cells, sides, width):
    for axis, dim in sides:
        count = lax.axis_size(axis)
        head = lax.slice_in_dim(cells, 0, width, axis=dim)
        tail = lax.slice_in_dim(cells, cells.shape[dim] - width, cells.shape[dim], axis=dim)
        cells = jnp.concatenate(
            [
                lax.ppermute(tail, axis, [(i, (i + 1) % count) for i in range(count)]),
                cells,
                lax.ppermute(head, axis, [((i + 1) % count, i) for i in range(count)]),
            ],
            axis=dim,
        )
    return cells


def lagrange_value(gll_nodes, node_index, point):
    value = 1.0
    for other_index in range(4):
        if other_index != node_index:
            value = (
                value
                * (point - gll_nodes[other_index])
                / (gll_nodes[node_index] - gll_nodes[other_index])
            )
    return value


def remap_tables():
    gll_nodes = np.array([-1.0, -1.0 / np.sqrt(5.0), 1.0 / np.sqrt(5.0), 1.0])
    offset = 0.5 / np.sqrt(3.0)
    halves = np.zeros((2, 4))
    for node_index in range(4):
        left_sum = lagrange_value(gll_nodes, node_index, -0.5 - offset) + lagrange_value(
            gll_nodes, node_index, -0.5 + offset
        )
        right_sum = lagrange_value(gll_nodes, node_index, 0.5 - offset) + lagrange_value(
            gll_nodes, node_index, 0.5 + offset
        )
        halves[0, node_index] = 0.5 * left_sum
        halves[1, node_index] = 0.5 * right_sum
    cell_weights = (halves[None, :, None, :] * halves[:, None, :, None]).reshape(4, 16)
    interp_cols = np.stack([0.5 - gll_nodes, 0.5 + gll_nodes], axis=1)
    cell_to_node = (interp_cols[None, :, None, :] * interp_cols[:, None, :, None]).reshape(16, 4)
    node_x = np.tile(gll_nodes, 4)
    node_y = np.repeat(gll_nodes, 4)
    slope_weights = 0.5 * np.stack(
        [
            np.maximum(0.0, -node_x),
            np.maximum(0.0, node_x),
            np.maximum(0.0, -node_y),
            np.maximum(0.0, node_y),
        ],
        axis=1,
    )
    return (
        jnp.asarray(cell_weights, jnp.float32),
        jnp.asarray(cell_to_node, jnp.float32),
        jnp.asarray(slope_weights, jnp.float32),
    )


def to_cells(gll_state, metric):
    cell_weights, cell_to_node, slope_weights = remap_tables()
    weighted = cell_weights[:, :, None] * metric[None, :, :]
    cell_area = jnp.sum(weighted, axis=1)
    cell_mass = jnp.einsum("cne,flne->flce", weighted, gll_state, precision=lax.Precision.HIGHEST)
    return cell_mass / cell_area[None, None]


def physics(cell_values, relax_rate, forcing, field_mix):
    mixed_fields = jnp.einsum(
        "fg,g...->f...", field_mix, cell_values, precision=lax.Precision.HIGHEST
    )
    return relax_rate[None] * jnp.tanh(mixed_fields + forcing[None])


def to_nodes(tendency, neighbour_means):
    cell_weights, cell_to_node, slope_weights = remap_tables()
    own_mean = jnp.mean(tendency, axis=2)
    reconstructed = jnp.einsum(
        "nc,flce->flne", cell_to_node, tendency, precision=lax.Precision.HIGHEST
    )
    reconstructed = reconstructed + jnp.einsum(
        "nk,flke->flne",
        slope_weights,
        neighbour_means - own_mean[:, :, None],
        precision=lax.Precision.HIGHEST,
    )
    lower_bound = jnp.minimum(jnp.min(tendency, axis=2), jnp.min(neighbour_means, axis=2))
    upper_bound = jnp.maximum(jnp.max(tendency, axis=2), jnp.max(neighbour_means, axis=2))
    return jnp.clip(reconstructed, lower_bound[:, :, None], upper_bound[:, :, None])


def on_device(gll_state, metric, phys_owner, neighbours, phys_rate, phys_forcing, field_mix):
    field_count, level_count, node_count, elem_count = gll_state.shape
    grp_size = lax.axis_size("grp")
    row_size = lax.axis_size("row")
    capacity = phys_rate.shape[1] // grp_size
    cell_values = to_cells(gll_state, metric)
    column_cells = cell_values.transpose(0, 1, 3, 2).reshape(
        field_count, level_count, 4 * elem_count
    )
    owner_grp = phys_owner[:, :, 0].reshape(4 * elem_count)
    onehot = (owner_grp[:, None] == jnp.arange(grp_size, dtype=jnp.int32)[None, :]).astype(
        jnp.int32
    )
    slot_rank = jnp.sum((jnp.cumsum(onehot, axis=0) - onehot) * onehot, axis=1)
    target = owner_grp * capacity + slot_rank
    rate_slots, forcing_slots = (
        lax.all_to_all(
            phys_rate.reshape(level_count, grp_size, capacity),
            "grp",
            split_axis=1,
            concat_axis=1,
            tiled=True,
        ),
        lax.all_to_all(
            phys_forcing.reshape(level_count, grp_size, capacity),
            "grp",
            split_axis=1,
            concat_axis=1,
            tiled=True,
        ),
    )
    relax_rate = rate_slots.reshape(level_count, grp_size * capacity)[:, target]
    forcing = forcing_slots.reshape(level_count, grp_size * capacity)[:, target]
    column_tend = physics(column_cells, relax_rate, forcing, field_mix)
    tendency = column_tend.reshape(field_count, level_count, elem_count, 4).transpose(0, 1, 3, 2)
    own_mean = jnp.mean(tendency, axis=2).reshape(field_count * level_count, elem_count)
    padded = padded_2(own_mean, ((("grp", "row"), 1),), HALO)
    total_elems = elem_count * grp_size * row_size
    first_elem = (lax.axis_index("grp") * row_size + lax.axis_index("row")) * elem_count
    local_index = (neighbours - first_elem + HALO) % total_elems
    neighbour_means = jnp.take(padded, local_index, axis=1).reshape(
        field_count, level_count, 4, elem_count
    )
    return to_nodes(tendency, neighbour_means)


def solution(mesh):
    in_specs = (
        P(None, None, None, ("grp", "row")),
        P(None, ("grp", "row")),
        P(("grp", "row"), None, None),
        P(None, ("grp", "row")),
        P(None, ("grp", "row")),
        P(None, ("grp", "row")),
        P(),
    )
    out_specs = P(None, None, None, ("grp", "row"))
    return jax.shard_map(
        on_device, mesh=mesh, in_specs=in_specs, out_specs=out_specs, check_vma=False
    )
```

profile of v0, /device:TPU:0, one launch (start us, length us, event | category | flops | bytes accessed | tf_op | source)
XLA Modules:
  0.0 66.3 jit_solution(11681408883932094924)
XLA Ops:
  0.0 0.9 %copy-done = f32[32,1024]{1,0:T(8,128)S(1)} copy-done((f32[32,1024]{1,0:T(8,128)S(1)}, f32[32,1024]{1,0:T(8,128)}, u32[]{:S(2)}) %copy-start) | copy-done | bytes 131096
  0.9 0.7 copy_bitcast_fusion
  1.6 7.3 %all-to-all-start.1 = ((f32[32,8,128]{2,0,1:T(8,128)}), f32[32,8,128]{2,0,1:T(8,128)S(1)}, u32[]{:S(2)}, u32[]{:S(2)}) async-start(f32[32,8,128]{2,0,1:T(8,128)} %copy_bitcast_fusion), calls=%async_computation.1 | async-start | bytes 262144 | tf_op jit(solution)/shard_map/all_to_all | solution.py:127
  8.8 0.7 %broadcast_multiply_fusion.1 = s32[128,4,1]{0,2,1:T(1,128)S(1)} fusion(s32[128,4,1]{0,2,1:T(1,128)} %param.12), kind=kLoop, calls=%fused_computation.39 | loop fusion | flops 512 | bytes 4096 | tf_op jit(solution)/shard_map/mul | solution.py:118
  9.5 0.8 %copy.91 = s32[128,4,1]{1,0,2:T(8,128)S(1)} copy(s32[128,4,1]{0,2,1:T(1,128)} %param.12) | data formatting | bytes 4096 | tf_op args[2]
  10.3 0.1 eq.31
  10.4 0.1 eq.27
  10.6 0.0 copy-start.6
  10.6 8.4 %copy.95 = f32[8,32,16,128]{1,2,0,3:T(8,128)} copy(f32[8,32,16,128]{3,2,1,0:T(8,128)} %param.10) | data formatting | bytes 4194304 | tf_op args[0]
  19.0 0.1 copy.94
  19.1 0.1 copy.90
  19.2 0.1 mul.51
  19.3 1.1 %reduce-window.6 = s32[8,4,128]{2,0,1:T(8,128)S(1)} reduce-window(s32[8,4,128]{2,0,1:T(8,128)S(1)} %fusion.10, s32[]{:T(128)} %constant.29.clone.1), window={size=1x1x128 pad=0_0x0_0x127_0}, to_apply=%region_0.0 | reduce-window | flops 520192 | bytes 32772 | tf_op jit(solution)/shard_map/reduce-window
  20.4 0.2 slice_reduce_fusion
  20.7 0.2 multiply_reduce_fusion
  20.9 7.6 %divide_bitcast_fusion = f32[8,32,128,4]{1,3,0,2:T(4,128)} fusion(f32[8,32,16,128]{1,2,0,3:T(8,128)} %copy.95, f32[128,4]{1,0:T(8,128)S(1)} %bitcast.87, f32[16,128]{0,1:T(8,128)S(1)} %copy.94, f32[4,16]{1,0:T(4,128)S(1)} %copy-done.6), kind=kOutput, calls=%fused_computation.4 | convolution fusion | flops 25305088 | bytes 2631936 | tf_op jit(solution)/shard_map/cne,flne->flce/dot_general | solution.py:76
  28.5 0.1 fusion.9
  28.6 0.6 copy_bitcast_fusion.1
  29.3 6.0 %all-to-all-start = ((f32[32,8,128]{2,0,1:T(8,128)}), f32[32,8,128]{2,0,1:T(8,128)S(1)}, u32[]{:S(2)}, u32[]{:S(2)}) async-start(f32[32,8,128]{2,0,1:T(8,128)} %copy_bitcast_fusion.1), calls=%async_computation | async-start | bytes 262144 | tf_op jit(solution)/shard_map/all_to_all | solution.py:120
  35.3 1.8 %copy.96 = f32[8,32,128,4]{1,0,3,2:T(8,128)S(1)} copy(f32[8,32,128,4]{1,3,0,2:T(4,128)} %divide_bitcast_fusion) | data formatting | bytes 1048576 | tf_op jit(solution)/shard_map/div | solution.py:77
  37.1 0.9 %copy.97 = f32[8,32,512]{2,0,1:T(8,128)S(1)} copy(f32[8,32,512]{1,0,2:T(8,128)S(1)} %bitcast.77) | data formatting | bytes 1048576 | tf_op jit(solution)/shard_map/reshape | solution.py:110
  38.0 0.2 copy.99
  38.2 1.0 %gather_fusion.1 = f32[512,32]{1,0:T(8,128)S(1)} fusion(f32[32,1024]{0,1:T(8,128)S(1)} %bitcast.81, s32[1024]{0:T(1024)S(1)} %pad_clamp_fusion.1), kind=kCustom, calls=%fused_computation.1 | custom fusion | bytes 133120 | tf_op jit(solution)/shard_map/gather | solution.py:136
  39.3 0.1 copy.100
  39.4 3.2 %all-to-all-done = f32[32,8,128]{2,0,1:T(8,128)S(1)} async-done(((f32[32,8,128]{2,0,1:T(8,128)}), f32[32,8,128]{2,0,1:T(8,128)S(1)}, u32[]{:S(2)}, u32[]{:S(2)}) %all-to-all-start) | async-done | bytes 131104 | tf_op jit(solution)/shard_map/all_to_all | solution.py:120
  42.6 0.2 copy.89
  42.8 1.0 %gather_fusion = f32[512,32]{1,0:T(8,128)S(1)} fusion(f32[32,1024]{0,1:T(8,128)S(1)} %bitcast.79, s32[1024]{0:T(1024)S(1)} %pad_clamp_fusion.1), kind=kCustom, calls=%fused_computation | custom fusion | bytes 133120 | tf_op jit(solution)/shard_map/gather | solution.py:135
  43.9 0.1 copy.93
  44.0 0.6 fusion.2
  44.6 0.8 %copy.101 = f32[8,32,512]{1,0,2:T(8,128)S(1)} copy(f32[8,32,512]{2,0,1:T(8,128)S(1)} %fusion.2) | data formatting | bytes 1048576 | tf_op jit(solution)/shard_map/mul | solution.py:84
  45.4 1.7 %bitcast_reduce_fusion.2 = (f32[8,32,128]{1,0,2:T(8,128)S(1)}, f32[8,32,128]{1,0,2:T(8,128)}, f32[8,32,128]{1,0,2:T(8,128)S(1)}) fusion(f32[8,32,512]{1,0,2:T(8,128)S(1)} %copy.101), kind=kLoop, calls=%fused_computation.42 | loop fusion | flops 294912 | bytes 917504 | tf_op jit(solution)/shard_map/reduce_max | solution.py:100
  47.1 2.1 %copy.113 = f32[8,32,4,128]{3,2,1,0:T(4,128)} copy(f32[8,32,4,128]{1,0,2,3:T(8,128)S(1)} %bitcast.76) | data formatting | bytes 1048576 | tf_op jit(solution)/shard_map/transpose | solution.py:138
  49.1 1.2 %copy.102 = f32[8,32,128]{2,1,0:T(8,128)S(1)} copy(f32[8,32,128]{1,0,2:T(8,128)} %get-tuple-element.6) | data formatting | bytes 262144 | tf_op jit(solution)/shard_map/reduce_sum | solution.py:139
  50.4 0.1 copy.103
  50.5 0.6 fusion.13
  51.1 0.8 %collective-permute-start.1 = (f32[256,32]{0,1:T(8,128)}, f32[256,32]{0,1:T(8,128)}, u32[]{:S(2)}, u32[]{:S(2)}) collective-permute-start(f32[256,32]{0,1:T(8,128)} %get-tuple-element.13), channel_id=1, source_target_pairs={{1,0},{2,1},{3,2},{4,3},{5,4},{6,5},{7,6},{8,7},{9,8},{10,9},{11,1... | collective-permute-start | bytes 98312 | tf_op jit(solution)/shard_map/ppermute | solution.py:19
  51.9 2.9 %fusion.14 = f32[8,32,128,16]{2,3,1,0:T(8,128)S(1)} fusion(f32[8,32,4,128]{3,2,1,0:T(4,128)} %copy.113, f32[16,4,1,1]{0,1,3,2:T(4,128)S(1)} %copy-done.8), kind=kOutput, calls=%fused_computation.44 | convolution fusion | flops 25165824 | bytes 2621696 | tf_op jit(solution)/shard_map/nc,flce->flne/dot_general | solution.py:90
  54.8 0.9 %copy.112 = f32[8,32,128]{2,1,0:T(8,128)} copy(f32[8,32,128]{1,0,2:T(8,128)S(1)} %get-tuple-element.7) | data formatting | bytes 262144 | tf_op jit(solution)/shard_map/reduce_min | solution.py:99
  55.6 0.8 %copy.109 = f32[8,32,128]{2,1,0:T(8,128)} copy(f32[8,32,128]{1,0,2:T(8,128)S(1)} %get-tuple-element.5) | data formatting | bytes 262144 | tf_op jit(solution)/shard_map/reduce_max | solution.py:100
  56.5 2.7 %collective-permute-done = f32[256,32]{0,1:T(8,128)} collective-permute-done((f32[256,32]{0,1:T(8,128)}, f32[256,32]{0,1:T(8,128)}, u32[]{:S(2)}, u32[]{:S(2)}) %collective-permute-start) | collective-permute-done | bytes 32800 | tf_op jit(solution)/shard_map/ppermute | solution.py:17
  59.1 0.8 %pad_maximum_fusion = f32[256,192]{0,1:T(8,128)S(1)} fusion(f32[256,32]{0,1:T(8,128)} %collective-permute-done.1, f32[256,128]{0,1:T(8,128)S(1)} %copy.103, f32[256,32]{0,1:T(8,128)} %collective-permute-done), kind=kLoop, calls=%fused_computation.16 | loop fusion | flops 98304 | bytes 393216 | tf_op jit(solution)/shard_map/concatenate | solution.py:15
  59.9 1.6 %gather_fusion.2 = f32[512,256]{1,0:T(8,128)S(1)} fusion(f32[256,192]{0,1:T(8,128)S(1)} %pad_maximum_fusion, s32[1024]{0:T(1024)S(1)} %pad_clamp_fusion), kind=kCustom, calls=%fused_computation.2 | custom fusion | bytes 1050624 | tf_op jit(solution)/shard_map/jit(_take)/gather | solution.py:144
  61.5 0.0 copy-start.5
  61.5 0.2 copy.106
  61.7 0.1 fusion.4
  61.8 0.1 select_subtract_fusion
  61.8 0.9 %min.23 = f32[8,32,128]{2,1,0:T(8,128)S(1)} minimum(f32[8,32,128]{2,1,0:T(8,128)} %copy.112, f32[8,32,128]{2,1,0:T(8,128)S(1)} %bitcast.84) | non-fusion elementwise | flops 32768 | bytes 393216 | tf_op jit(solution)/shard_map/min | solution.py:99
  62.8 3.4 %minimum_bitcast_fusion = f32[8,32,16,128]{3,2,1,0:T(8,128)} fusion(f32[8,32,128,16]{2,3,1,0:T(8,128)S(1)} %fusion.14, f32[16,4,1,1]{0,1,3,2:T(4,128)S(1)} %copy-done.5, f32[8,32,128]{2,1,0:T(8,128)S(1)} %min.23, f32[8,32,128]{2,1,0:T(8,128)S(1)} %max.20, f32[8,32,4,128]{3,1,0,2:T(8,128)S(1)} %select_subtract_fusion), kind=kOutput, calls=%fused_computation.3 | convolution fusion | flops 26738688 | bytes 4980992 | tf_op jit(solution)/shard_map/nk,flke->flne/dot_general | solution.py:93
  (27 shorter events, 0.2 us)
Async XLA Ops:
  0.0 0.9 %copy-start = (f32[32,1024]{1,0:T(8,128)S(1)}, f32[32,1024]{1,0:T(8,128)}, u32[]{:S(2)}) copy-start(f32[32,1024]{1,0:T(8,128)} %param.15) | copy-start | bytes 393220
  1.6 27.7 %all-to-all-start.1 = ((f32[32,8,128]{2,0,1:T(8,128)}), f32[32,8,128]{2,0,1:T(8,128)S(1)}, u32[]{:S(2)}, u32[]{:S(2)}) async-start(f32[32,8,128]{2,0,1:T(8,128)} %copy_bitcast_fusion), calls=%async_computation.1 | async-start | bytes 262144 | tf_op jit(solution)/shard_map/all_to_all | solution.py:127
  10.5 8.4 %copy-start.3 = (f32[16,128]{1,0:T(8,128)S(1)}, f32[16,128]{1,0:T(8,128)}, u32[]{:S(2)}) copy-start(f32[16,128]{1,0:T(8,128)} %param.11) | copy-start | bytes 24580
  10.6 10.1 %copy-start.6 = (f32[4,16]{1,0:T(4,128)S(1)}, f32[4,16]{1,0:T(4,128)}, u32[]{:S(2)}) copy-start(f32[4,16]{1,0:T(4,128)} %constant.69.clone) | copy-start | bytes 772
  20.9 7.7 %copy-start.2 = (f32[32,1024]{1,0:T(8,128)S(1)}, f32[32,1024]{1,0:T(8,128)}, u32[]{:S(2)}) copy-start(f32[32,1024]{1,0:T(8,128)} %param.14) | copy-start | bytes 393220
  20.9 14.3 %copy-start.7 = (s32[4,128]{1,0:T(4,128)S(1)}, s32[4,128]{1,0:T(4,128)}, u32[]{:S(2)}) copy-start(s32[4,128]{1,0:T(4,128)} %param.13) | copy-start | bytes 6148
  29.3 13.3 %all-to-all-start = ((f32[32,8,128]{2,0,1:T(8,128)}), f32[32,8,128]{2,0,1:T(8,128)S(1)}, u32[]{:S(2)}, u32[]{:S(2)}) async-start(f32[32,8,128]{2,0,1:T(8,128)} %copy_bitcast_fusion.1), calls=%async_computation | async-start | bytes 262144 | tf_op jit(solution)/shard_map/all_to_all | solution.py:120
  38.0 6.0 %copy-start.4 = (f32[8,8]{1,0:T(8,128)S(1)}, f32[8,8]{1,0:T(8,128)}, u32[]{:S(2)}) copy-start(f32[8,8]{1,0:T(8,128)} %param.16) | copy-start | bytes 772
  47.1 4.8 %copy-start.8 = (f32[16,4,1,1]{0,1,3,2:T(4,128)S(1)}, f32[16,4,1,1]{0,1,3,2:T(4,128)}, u32[]{:S(2)}) copy-start(f32[16,4,1,1]{0,1,3,2:T(4,128)} %constant.72) | copy-start | bytes 772
  51.1 5.4 %collective-permute-start.1 = (f32[256,32]{0,1:T(8,128)}, f32[256,32]{0,1:T(8,128)}, u32[]{:S(2)}, u32[]{:S(2)}) collective-permute-start(f32[256,32]{0,1:T(8,128)} %get-tuple-element.13), channel_id=1, source_target_pairs={{1,0},{2,1},{3,2},{4,3},{5,4},{6,5},{7,6},{8,7},{9,8},{10,9},{11,1... | collective-permute-start | bytes 98312 | tf_op jit(solution)/shard_map/ppermute | solution.py:19
  51.9 7.3 %collective-permute-start = (f32[256,32]{0,1:T(8,128)}, f32[256,32]{0,1:T(8,128)}, u32[]{:S(2)}, u32[]{:S(2)}) collective-permute-start(f32[256,32]{0,1:T(8,128)} %get-tuple-element.12), channel_id=1, source_target_pairs={{0,1},{1,2},{2,3},{3,4},{4,5},{5,6},{6,7},{7,8},{8,9},{9,10},{10,1... | collective-permute-start | bytes 98312 | tf_op jit(solution)/shard_map/ppermute | solution.py:17
  61.5 1.3 %copy-start.1 = (f32[8,32,128]{2,1,0:T(8,128)S(1)}, f32[8,32,128]{2,1,0:T(8,128)}, u32[]{:S(2)}) copy-start(f32[8,32,128]{2,1,0:T(8,128)} %copy.109) | copy-start | bytes 393220
  61.5 1.3 %copy-start.5 = (f32[16,4,1,1]{0,1,3,2:T(4,128)S(1)}, f32[16,4,1,1]{0,1,3,2:T(4,128)}, u32[]{:S(2)}) copy-start(f32[16,4,1,1]{0,1,3,2:T(4,128)} %constant.73) | copy-start | bytes 772
where the time goes:
time: 66.8 us; the launch traced here: 66.3 us
  local copies, waits for them, and re-layouts  25.8 us (39%)
  matrix products  14.5 us (22%)
  starting transfers between devices  14 us (21%)
  waiting for transfers between devices  5.89 us (9%)
  other arithmetic  5.73 us (9%)
    unnamed x21, local copies, waits for them, and re-layouts  10.2 us
    dot_general x1, matrix products, to_cells(): jnp.einsum('cne,flne->flce', weighted, gll_state, precision=lax.Precision...  7.56 us
    all_to_all x1, starting transfers between devices, on_device(): lax.all_to_all(phys_forcing.reshape(level_count, grp_size, capacity), 'gr...  7.28 us
    all_to_all x1, starting transfers between devices, on_device(): lax.all_to_all(phys_rate.reshape(level_count, grp_size, capacity), 'grp',...  6 us
    dot_general x1, matrix products, to_nodes(): jnp.einsum('nk,flke->flne', slope_weights, neighbour_means - own_mean[:,...  3.44 us
    all_to_all x1, waiting for transfers between devices, on_device(): lax.all_to_all(phys_rate.reshape(level_count, grp_size, capacity), 'grp',...  3.24 us
    dot_general x1, matrix products, to_nodes(): jnp.einsum('nc,flce->flne', cell_to_node, tendency, precision=lax.Precisi...  2.87 us
    ppermute x1, waiting for transfers between devices, padded_2(): lax.ppermute(tail, axis, [(i, (i + 1) % count) for i in range(count)])  2.65 us
  transfers between devices with their start and end apart: 4, of which 2 were waited for; matrix products, arithmetic and copies ran while one was open for 44% of the time, Pallas kernels for 0%

commit v1 on v0

--- a/solution.py
+++ b/solution.py
@@ -124,12 +124,20 @@
             concat_axis=1,
             tiled=True,
         ),
-        lax.all_to_all(
-            phys_forcing.reshape(level_count, grp_size, capacity),
-            "grp",
-            split_axis=1,
-            concat_axis=1,
-            tiled=True,
+        jnp.concatenate(
+            lax.all_to_all(
+                jnp.stack(
+                    jnp.split(
+                        phys_forcing.reshape(level_count, grp_size, capacity),
+                        lax.axis_size("grp"),
+                        axis=1,
+                    )
+                ),
+                "grp",
+                0,
+                0,
+            ),
+            axis=1,
         ),
     )
     relax_rate = rate_slots.reshape(level_count, grp_size * capacity)[:, target]

time: 66.8 us -> 71.1 us (1.064)
  local copies, waits for them, and re-layouts: 25.8 us -> 30.1 us
    unnamed x21 -> x27, local copies, waits for them, and re-layouts: 10.2 us -> 14.5 us
  transfers between devices with their start and end apart: 4 -> 4, of which waited for: 2 -> 2; matrix products, arithmetic and copies ran while one was open for 44% -> 41% of each run, Pallas kernels for 0% -> 0%
where the time goes in v1:
time: 71.1 us; the launch traced here: 70.5 us
  local copies, waits for them, and re-layouts  30.1 us (42%)
  matrix products  14.4 us (20%)
  starting transfers between devices  14 us (20%)
  waiting for transfers between devices  5.89 us (8%)
  other arithmetic  5.73 us (8%)
    unnamed x27, local copies, waits for them, and re-layouts  14.5 us
    dot_general x1, matrix products, to_cells(): jnp.einsum('cne,flne->flce', weighted, gll_state, precision=lax.Precision...  7.51 us
    all_to_all x1, starting transfers between devices, on_device(): lax.all_to_all(jnp.stack(jnp.split(phys_forcing.reshape(level_count, grp_...  7.28 us
    all_to_all x1, starting transfers between devices, on_device(): lax.all_to_all(phys_rate.reshape(level_count, grp_size, capacity), 'grp',...  6 us
    dot_general x1, matrix products, to_nodes(): jnp.einsum('nk,flke->flne', slope_weights, neighbour_means - own_mean[:,...  3.44 us
    all_to_all x1, waiting for transfers between devices, on_device(): lax.all_to_all(phys_rate.reshape(level_count, grp_size, capacity), 'grp',...  3.24 us
    dot_general x1, matrix products, to_nodes(): jnp.einsum('nc,flce->flne', cell_to_node, tendency, precision=lax.Precisi...  2.87 us
    ppermute x1, waiting for transfers between devices, padded_2(): lax.ppermute(tail, axis, [(i, (i + 1) % count) for i in range(count)])  2.65 us
  transfers between devices with their start and end apart: 4, of which 2 were waited for; matrix products, arithmetic and copies ran while one was open for 41% of the time, Pallas kernels for 0%

profile of v1, /device:TPU:0, one launch (start us, length us, event | category | flops | bytes accessed | tf_op | source)
XLA Modules:
  0.0 70.5 jit_solution(3568819752182827030)
XLA Ops:
  0.0 1.0 %copy.133 = f32[4,8,8,128]{3,2,1,0:T(8,128)S(1)} copy(f32[4,8,8,128]{3,1,2,0:T(8,128)} %bitcast.95) | data formatting | bytes 262144
  1.1 0.6 constant_dynamic-update-slice_fusion.7
  1.7 0.6 constant_dynamic-update-slice_fusion.6
  2.3 0.6 constant_dynamic-update-slice_fusion.5
  2.9 0.6 constant_dynamic-update-slice_fusion.4
  3.5 0.6 constant_dynamic-update-slice_fusion.3
  4.1 0.6 constant_dynamic-update-slice_fusion.2
  4.7 0.6 constant_dynamic-update-slice_fusion.1
  5.3 0.6 constant_dynamic-update-slice_fusion
  5.9 7.3 %all-to-all-start.1 = ((f32[8,32,1,128]{3,1,2,0:T(8,128)}), f32[8,32,1,128]{3,1,2,0:T(8,128)S(1)}, u32[]{:S(2)}, u32[]{:S(2)}) async-start(f32[8,32,1,128]{3,1,2,0:T(8,128)} %constant_dynamic-update-slice_fusion), calls=%async_computation.1 | async-start | bytes 262144 | tf_op jit(solution)/shard_map/all_to_all | solution.py:128
  13.2 0.7 broadcast_multiply_fusion.1
  13.8 0.8 %copy.104 = s32[128,4,1]{1,0,2:T(8,128)S(1)} copy(s32[128,4,1]{0,2,1:T(1,128)} %param.12) | data formatting | bytes 4096 | tf_op args[2]
  14.6 0.1 eq.31
  14.7 0.1 eq.27
  14.9 8.4 %copy.108 = f32[8,32,16,128]{1,2,0,3:T(8,128)} copy(f32[8,32,16,128]{3,2,1,0:T(8,128)} %param.10) | data formatting | bytes 4194304 | tf_op args[0]
  23.4 0.1 copy.103
  23.5 0.1 mul.51
  23.6 1.1 %reduce-window.6 = s32[8,4,128]{2,0,1:T(8,128)S(1)} reduce-window(s32[8,4,128]{2,0,1:T(8,128)S(1)} %fusion.10, s32[]{:T(128)} %constant.29.clone.1), window={size=1x1x128 pad=0_0x0_0x127_0}, to_apply=%region_0.0 | reduce-window | flops 520192 | bytes 32772 | tf_op jit(solution)/shard_map/reduce-window
  24.7 0.2 slice_reduce_fusion
  25.0 0.2 multiply_reduce_fusion
  25.2 7.5 %divide_bitcast_fusion = f32[8,32,128,4]{1,3,0,2:T(4,128)} fusion(f32[8,32,16,128]{1,2,0,3:T(8,128)} %copy.108, f32[128,4]{1,0:T(8,128)S(1)} %bitcast.104, f32[16,128]{0,1:T(8,128)S(1)} %copy.107, f32[4,16]{1,0:T(4,128)S(1)} %copy-done.5), kind=kOutput, calls=%fused_computation.4 | convolution fusion | flops 25305088 | bytes 2631936 | tf_op jit(solution)/shard_map/cne,flne->flce/dot_general | solution.py:76
  32.9 0.6 copy_bitcast_fusion
  33.5 6.0 %all-to-all-start = ((f32[32,8,128]{2,0,1:T(8,128)}), f32[32,8,128]{2,0,1:T(8,128)S(1)}, u32[]{:S(2)}, u32[]{:S(2)}) async-start(f32[32,8,128]{2,0,1:T(8,128)} %copy_bitcast_fusion), calls=%async_computation | async-start | bytes 262144 | tf_op jit(solution)/shard_map/all_to_all | solution.py:120
  39.5 1.8 %copy.109 = f32[8,32,128,4]{1,0,3,2:T(8,128)S(1)} copy(f32[8,32,128,4]{1,3,0,2:T(4,128)} %divide_bitcast_fusion) | data formatting | bytes 1048576 | tf_op jit(solution)/shard_map/div | solution.py:77
  41.3 0.9 %copy.110 = f32[8,32,512]{2,0,1:T(8,128)S(1)} copy(f32[8,32,512]{1,0,2:T(8,128)S(1)} %bitcast.83) | data formatting | bytes 1048576 | tf_op jit(solution)/shard_map/reshape | solution.py:110
  42.3 0.2 copy.111
  42.5 1.0 %gather_fusion.1 = f32[512,32]{1,0:T(8,128)S(1)} fusion(f32[32,1024]{0,1:T(8,128)S(1)} %bitcast.87, s32[1024]{0:T(1024)S(1)} %pad_clamp_fusion.1), kind=kCustom, calls=%fused_computation.1 | custom fusion | bytes 133120 | tf_op jit(solution)/shard_map/gather | solution.py:144
  43.5 0.1 copy.112
  43.6 3.2 %all-to-all-done = f32[32,8,128]{2,0,1:T(8,128)S(1)} async-done(((f32[32,8,128]{2,0,1:T(8,128)}), f32[32,8,128]{2,0,1:T(8,128)S(1)}, u32[]{:S(2)}, u32[]{:S(2)}) %all-to-all-start) | async-done | bytes 131104 | tf_op jit(solution)/shard_map/all_to_all | solution.py:120
  46.9 0.2 copy.102
  47.1 1.0 %gather_fusion = f32[512,32]{1,0:T(8,128)S(1)} fusion(f32[32,1024]{0,1:T(8,128)S(1)} %bitcast.85, s32[1024]{0:T(1024)S(1)} %pad_clamp_fusion.1), kind=kCustom, calls=%fused_computation | custom fusion | bytes 133120 | tf_op jit(solution)/shard_map/gather | solution.py:143
  48.1 0.1 copy.106
  48.2 0.6 fusion.2
  48.8 0.8 %copy.113 = f32[8,32,512]{1,0,2:T(8,128)S(1)} copy(f32[8,32,512]{2,0,1:T(8,128)S(1)} %fusion.2) | data formatting | bytes 1048576 | tf_op jit(solution)/shard_map/mul | solution.py:84
  49.7 1.7 %bitcast_reduce_fusion.2 = (f32[8,32,128]{1,0,2:T(8,128)S(1)}, f32[8,32,128]{1,0,2:T(8,128)}, f32[8,32,128]{1,0,2:T(8,128)S(1)}) fusion(f32[8,32,512]{1,0,2:T(8,128)S(1)} %copy.113), kind=kLoop, calls=%fused_computation.49 | loop fusion | flops 294912 | bytes 917504 | tf_op jit(solution)/shard_map/reduce_max | solution.py:100
  51.3 2.1 %copy.125 = f32[8,32,4,128]{3,2,1,0:T(4,128)} copy(f32[8,32,4,128]{1,0,2,3:T(8,128)S(1)} %bitcast.82) | data formatting | bytes 1048576 | tf_op jit(solution)/shard_map/transpose | solution.py:146
  53.4 1.2 %copy.114 = f32[8,32,128]{2,1,0:T(8,128)S(1)} copy(f32[8,32,128]{1,0,2:T(8,128)} %get-tuple-element.6) | data formatting | bytes 262144 | tf_op jit(solution)/shard_map/reduce_sum | solution.py:147
  54.7 0.6 fusion.13
  55.4 0.8 %collective-permute-start.1 = (f32[256,32]{0,1:T(8,128)}, f32[256,32]{0,1:T(8,128)}, u32[]{:S(2)}, u32[]{:S(2)}) collective-permute-start(f32[256,32]{0,1:T(8,128)} %get-tuple-element.13), channel_id=1, source_target_pairs={{1,0},{2,1},{3,2},{4,3},{5,4},{6,5},{7,6},{8,7},{9,8},{10,9},{11,1... | collective-permute-start | bytes 98312 | tf_op jit(solution)/shard_map/ppermute | solution.py:19
  56.1 2.9 %fusion.15 = f32[8,32,128,16]{2,3,1,0:T(8,128)S(1)} fusion(f32[8,32,4,128]{3,2,1,0:T(4,128)} %copy.125, f32[16,4,1,1]{0,1,3,2:T(4,128)S(1)} %copy-done.7), kind=kOutput, calls=%fused_computation.52 | convolution fusion | flops 25165824 | bytes 2621696 | tf_op jit(solution)/shard_map/nc,flce->flne/dot_general | solution.py:90
  59.0 0.9 %copy.124 = f32[8,32,128]{2,1,0:T(8,128)} copy(f32[8,32,128]{1,0,2:T(8,128)S(1)} %get-tuple-element.7) | data formatting | bytes 262144 | tf_op jit(solution)/shard_map/reduce_min | solution.py:99
  59.9 0.8 %copy.121 = f32[8,32,128]{2,1,0:T(8,128)} copy(f32[8,32,128]{1,0,2:T(8,128)S(1)} %get-tuple-element.5) | data formatting | bytes 262144 | tf_op jit(solution)/shard_map/reduce_max | solution.py:100
  60.7 2.6 %collective-permute-done = f32[256,32]{0,1:T(8,128)} collective-permute-done((f32[256,32]{0,1:T(8,128)}, f32[256,32]{0,1:T(8,128)}, u32[]{:S(2)}, u32[]{:S(2)}) %collective-permute-start) | collective-permute-done | bytes 32800 | tf_op jit(solution)/shard_map/ppermute | solution.py:17
  63.4 0.8 %pad_maximum_fusion = f32[256,192]{0,1:T(8,128)S(1)} fusion(f32[256,32]{0,1:T(8,128)} %collective-permute-done.1, f32[256,128]{0,1:T(8,128)S(1)} %copy.115, f32[256,32]{0,1:T(8,128)} %collective-permute-done), kind=kLoop, calls=%fused_computation.16 | loop fusion | flops 98304 | bytes 393216 | tf_op jit(solution)/shard_map/concatenate | solution.py:15
  64.2 1.6 %gather_fusion.2 = f32[512,256]{1,0:T(8,128)S(1)} fusion(f32[256,192]{0,1:T(8,128)S(1)} %pad_maximum_fusion, s32[1024]{0:T(1024)S(1)} %pad_clamp_fusion), kind=kCustom, calls=%fused_computation.2 | custom fusion | bytes 1050624 | tf_op jit(solution)/shard_map/jit(_take)/gather | solution.py:152
  65.8 0.2 copy.118
  66.1 0.9 %min.23 = f32[8,32,128]{2,1,0:T(8,128)S(1)} minimum(f32[8,32,128]{2,1,0:T(8,128)} %copy.124, f32[8,32,128]{2,1,0:T(8,128)S(1)} %bitcast.92) | non-fusion elementwise | flops 32768 | bytes 393216 | tf_op jit(solution)/shard_map/min | solution.py:99
  67.1 3.4 %minimum_bitcast_fusion = f32[8,32,16,128]{3,2,1,0:T(8,128)} fusion(f32[8,32,128,16]{2,3,1,0:T(8,128)S(1)} %fusion.15, f32[16,4,1,1]{0,1,3,2:T(4,128)S(1)} %copy-done.4, f32[8,32,128]{2,1,0:T(8,128)S(1)} %min.23, f32[8,32,128]{2,1,0:T(8,128)S(1)} %max.20, f32[8,32,4,128]{3,1,0,2:T(8,128)S(1)} %select_subtract_fusion), kind=kOutput, calls=%fused_computation.3 | convolution fusion | flops 26738688 | bytes 4980992 | tf_op jit(solution)/shard_map/nk,flke->flne/dot_general | solution.py:93
  (34 shorter events, 0.7 us)
Async XLA Ops:
  0.0 32.9 %copy-start = (f32[32,1024]{1,0:T(8,128)S(1)}, f32[32,1024]{1,0:T(8,128)}, u32[]{:S(2)}) copy-start(f32[32,1024]{1,0:T(8,128)} %param.14) | copy-start | bytes 393220
  5.9 27.6 %all-to-all-start.1 = ((f32[8,32,1,128]{3,1,2,0:T(8,128)}), f32[8,32,1,128]{3,1,2,0:T(8,128)S(1)}, u32[]{:S(2)}, u32[]{:S(2)}) async-start(f32[8,32,1,128]{3,1,2,0:T(8,128)} %constant_dynamic-update-slice_fusion), calls=%async_computation.1 | async-start | bytes 262144 | tf_op jit(solution)/shard_map/all_to_all | solution.py:128
  14.8 8.4 %copy-start.2 = (f32[16,128]{1,0:T(8,128)S(1)}, f32[16,128]{1,0:T(8,128)}, u32[]{:S(2)}) copy-start(f32[16,128]{1,0:T(8,128)} %param.11) | copy-start | bytes 24580
  14.9 10.1 %copy-start.5 = (f32[4,16]{1,0:T(4,128)S(1)}, f32[4,16]{1,0:T(4,128)}, u32[]{:S(2)}) copy-start(f32[4,16]{1,0:T(4,128)} %constant.69.clone) | copy-start | bytes 772
  25.2 14.3 %copy-start.6 = (s32[4,128]{1,0:T(4,128)S(1)}, s32[4,128]{1,0:T(4,128)}, u32[]{:S(2)}) copy-start(s32[4,128]{1,0:T(4,128)} %param.13) | copy-start | bytes 6148
  33.5 13.3 %all-to-all-start = ((f32[32,8,128]{2,0,1:T(8,128)}), f32[32,8,128]{2,0,1:T(8,128)S(1)}, u32[]{:S(2)}, u32[]{:S(2)}) async-start(f32[32,8,128]{2,0,1:T(8,128)} %copy_bitcast_fusion), calls=%async_computation | async-start | bytes 262144 | tf_op jit(solution)/shard_map/all_to_all | solution.py:120
  42.2 6.0 %copy-start.3 = (f32[8,8]{1,0:T(8,128)S(1)}, f32[8,8]{1,0:T(8,128)}, u32[]{:S(2)}) copy-start(f32[8,8]{1,0:T(8,128)} %param.16) | copy-start | bytes 772
  51.3 4.8 %copy-start.7 = (f32[16,4,1,1]{0,1,3,2:T(4,128)S(1)}, f32[16,4,1,1]{0,1,3,2:T(4,128)}, u32[]{:S(2)}) copy-start(f32[16,4,1,1]{0,1,3,2:T(4,128)} %constant.72) | copy-start | bytes 772
  55.4 5.4 %collective-permute-start.1 = (f32[256,32]{0,1:T(8,128)}, f32[256,32]{0,1:T(8,128)}, u32[]{:S(2)}, u32[]{:S(2)}) collective-permute-start(f32[256,32]{0,1:T(8,128)} %get-tuple-element.13), channel_id=1, source_target_pairs={{1,0},{2,1},{3,2},{4,3},{5,4},{6,5},{7,6},{8,7},{9,8},{10,9},{11,1... | collective-permute-start | bytes 98312 | tf_op jit(solution)/shard_map/ppermute | solution.py:19
  56.1 7.3 %collective-permute-start = (f32[256,32]{0,1:T(8,128)}, f32[256,32]{0,1:T(8,128)}, u32[]{:S(2)}, u32[]{:S(2)}) collective-permute-start(f32[256,32]{0,1:T(8,128)} %get-tuple-element.12), channel_id=1, source_target_pairs={{0,1},{1,2},{2,3},{3,4},{4,5},{5,6},{6,7},{7,8},{8,9},{9,10},{10,1... | collective-permute-start | bytes 98312 | tf_op jit(solution)/shard_map/ppermute | solution.py:17
  65.7 1.3 %copy-start.1 = (f32[8,32,128]{2,1,0:T(8,128)S(1)}, f32[8,32,128]{2,1,0:T(8,128)}, u32[]{:S(2)}) copy-start(f32[8,32,128]{2,1,0:T(8,128)} %copy.121) | copy-start | bytes 393220
  65.8 1.3 %copy-start.4 = (f32[16,4,1,1]{0,1,3,2:T(4,128)S(1)}, f32[16,4,1,1]{0,1,3,2:T(4,128)}, u32[]{:S(2)}) copy-start(f32[16,4,1,1]{0,1,3,2:T(4,128)} %constant.73) | copy-start | bytes 772
